TPU v7x, 32 devices: a whole 2x2x4 slice. The times are simulated.
32 devices in a mesh: attn: 4 (over y, x), expert: 8 (over z, core).
Axes of the slice: x: 2, y: 2, z: 4, core: 2. Of those that a mesh axis runs over, the one named last changes fastest.
Arguments:
- tokens: bfloat16 [1024, 2880], P(('attn', 'expert')), may hold values from -6 to 6
- expert_ids: int32 [1024, 4], P(('attn', 'expert')), may hold values from 0 to 7, all different within a row; in each aligned block of 32 rows (0 to 31, 32 to 63, ...) at most 32 rows name the same one
- gate_probs: float32 [1024, 4], P(('attn', 'expert')), may hold values from 0.05 to 0.6
- shed_blocks: int32 [8], replicated, may hold values from 0 to 4, as said below
- partner: int32 [8], replicated, may hold values from 0 to 7, as said below
- gate_weight: bfloat16 [8, 2880, 2880], P('expert', None, 'attn'), may hold values from -0.109375 to 0.109375
- up_weight: bfloat16 [8, 2880, 2880], P('expert', None, 'attn'), may hold values from -0.109375 to 0.109375
- down_weight: bfloat16 [8, 2880, 2880], P('expert', 'attn'), may hold values from -0.109375 to 0.109375
Outputs:
- moe_out: bfloat16 [1024, 2880], P(('attn', 'expert'))
Inputs may be any that keep to these rules, and one draw needn't show every extreme that they name: `expert_ids`: in the rows of one device, no expert is named by more than 32 rows; the 4 experts of a token differ. `shed_blocks`: some expert has exactly 4. partner pairs the experts: partner[partner[e]] = e and partner[e] != e.
All inputs are finite; a program needn't handle non-finite values.
Results may differ from a plain program's by a relative error of at most 0.0081.
Values may be sent and summed in bfloat16 or wider, within the bound.
A program may use at most 128 MiB of HBM per device.

v0:
```python
import jax
import jax.numpy as jnp
from jax import lax
from jax.sharding import PartitionSpec as P

SHED_MOST = 4
SWISH_SCALE = 1.702


def lookup(table, indices):
    places = jnp.arange(table.shape[0], dtype=jnp.int32)
    return jnp.sum(jnp.where(indices[:, None] == places[None, :], table[None, :], 0), axis=1)


def row_weights(all_ids, all_probs, shed_blocks, partner, capacity, block_size):
    me = lax.axis_index("expert").astype(jnp.int32)
    named = all_ids == me
    mask = jnp.any(named, axis=1).astype(jnp.int32)
    rank = jnp.cumsum(mask) - mask
    other = lookup(partner, me[None])
    bound = (
        capacity
        - block_size * lookup(shed_blocks, other)
        + block_size * lookup(shed_blocks, me[None])
    )
    weight = jnp.sum(jnp.where(named, all_probs, 0.0), axis=1)
    return jnp.where(rank < bound, weight, 0.0)


def on_device(
    tokens, expert_ids, gate_probs, shed_blocks, partner, gate_weight, up_weight, down_weight
):
    tok_rows, model_width = tokens.shape
    top_count = expert_ids.shape[1]
    capacity = tok_rows * top_count * lax.axis_size("attn")
    block_size = capacity // 8
    both = ("attn", "expert")
    all_ids = lax.all_gather(expert_ids, both, axis=0, tiled=True)
    all_probs = lax.all_gather(gate_probs, both, axis=0, tiled=True)
    rows = lax.all_gather(tokens, both, axis=0, tiled=True)
    weight = row_weights(all_ids, all_probs, shed_blocks, partner, capacity, block_size)
    gate_part = jnp.dot(rows, gate_weight[0], preferred_element_type=jnp.float32)
    up_part = jnp.dot(rows, up_weight[0], preferred_element_type=jnp.float32)
    hidden = gate_part * jax.nn.sigmoid(SWISH_SCALE * gate_part) * (up_part + 1.0)
    hidden = (hidden * weight[:, None]).astype(jnp.bfloat16)
    share = jnp.dot(hidden, down_weight[0], preferred_element_type=jnp.float32).astype(jnp.bfloat16)
    share = lax.psum_scatter(share, "attn", scatter_dimension=0, tiled=True)
    return lax.psum_scatter(share, "expert", scatter_dimension=0, tiled=True)


def solution(mesh):
    in_specs = (
        P(("attn", "expert"), None),
        P(("attn", "expert"), None),
        P(("attn", "expert"), None),
        P(),
        P(),
        P("expert", None, "attn"),
        P("expert", None, "attn"),
        P("expert", "attn", None),
    )
    out_specs = P(("attn", "expert"), None)
    return jax.shard_map(
        on_device, mesh=mesh, in_specs=in_specs, out_specs=out_specs, check_vma=False
    )
```

profile of v0, /device:TPU:0, one launch (start us, length us, event | category | flops | bytes accessed | tf_op | source)
XLA Modules:
  0.0 226.7 jit_solution(15309892988968563415)
XLA Ops:
  6.5 0.0 all-gather.4.cloned.1.call-start
  6.5 0.7 all-gather.4.cloned.1.call-update
  7.3 0.0 reduce-scatter.5.cloned.1.call-start
  7.3 44.1 %all-gather = s32[32,32,4]{1,2,0:T(4,128)S(1)} all-gather(s32[1,32,4]{1,2,0:T(4,128)} %bitcast.24), channel_id=1, replica_groups=mesh['attn'=4,'expert'=8] {'attn','expert'}, dimensions={0}, use_global_device_ids=true | all-gather | bytes 16896 | tf_op jit(solution)/shard_map/all_gather | solution.py:38
  51.4 0.1 fusion.19
  51.4 0.1 reshape.58
  51.5 0.1 reshape.68
  51.6 1.3 fusion.14
  52.9 2.0 fusion.15
  56.1 0.3 reduce-window.9
  56.4 0.1 slice.7
  56.5 37.9 %all-gather.1 = f32[32,32,4]{1,2,0:T(4,128)S(1)} all-gather(f32[1,32,4]{1,2,0:T(4,128)} %bitcast.25), channel_id=1, replica_groups=mesh['attn'=4,'expert'=8] {'attn','expert'}, dimensions={0}, use_global_device_ids=true | all-gather | bytes 16896 | tf_op jit(solution)/shard_map/all_gather | solution.py:39
  94.4 0.1 select_reduce_fusion
  94.5 0.1 reshape.70
  94.6 0.1 slice_reduce_fusion
  94.7 0.1 fusion.13
  94.8 0.0 all-gather.4.cloned.1.call-done
  94.8 8.1 %fusion.1 = f32[1024,720]{0,1:T(8,128)S(1)} fusion(bf16[1024,2880]{1,0:T(8,128)(2,1)} %all-gather.4.cloned.1.call-done, bf16[1,2880,720]{1,2,0:T(8,128)(2,1)} %param.14), kind=kOutput, calls=%fused_computation.2 | convolution fusion | flops 4246732800 | bytes 12994560 | tf_op jit(solution)/shard_map/dot_general | solution.py:43
  102.9 16.3 %convolution_convert_fusion = bf16[1024,2880]{0,1:T(8,128)(2,1)} fusion(bf16[1,720,2880]{2,1,0:T(8,128)(2,1)} %param.15, f32[1024,720]{0,1:T(8,128)S(1)} %fusion.1, bf16[1024,2880]{1,0:T(8,128)(2,1)} %all-gather.4.cloned.1.call-done, bf16[1,2880,720]{1,2,0:T(8,128)(2,1)} %param.13, f32[1024]{0:T(1024)S(1)} %fusion.13), kind=kOutput, calls=%fused_computation | convolution fusion | flops 8503050240 | bytes 23044096 | tf_op jit(solution)/shard_map/dot_general | solution.py:46
  119.1 0.0 reduce-scatter.5.cloned.1.call-update
  119.2 0.0 reduce-scatter.7.cloned.1.call-start
  119.2 64.1 %reduce-scatter.5.cloned.1.call-done = bf16[256,2880]{0,1:T(8,128)(2,1)} async-done(((bf16[1024,2880]{0,1:T(8,128)(2,1)}), bf16[256,2880]{0,1:T(8,128)(2,1)}) %reduce-scatter.5.cloned.1.call-update) | async-done | bytes 1474576 | tf_op jit(solution)/shard_map/reduce_scatter | solution.py:47
  183.3 2.6 %copy.12 = bf16[256,2880]{1,0:T(8,128)(2,1)} copy(bf16[256,2880]{0,1:T(8,128)(2,1)} %reduce-scatter.5.cloned.1.call-done) | data formatting | bytes 2949120
  185.9 0.0 reduce-scatter.7.cloned.1.call-update
  185.9 34.3 %reduce-scatter.7.cloned.1.call-done = bf16[32,2880]{1,0:T(8,128)(2,1)} async-done(((bf16[256,2880]{1,0:T(8,128)(2,1)}), bf16[32,2880]{1,0:T(8,128)(2,1)}) %reduce-scatter.7.cloned.1.call-update) | async-done | bytes 184336 | tf_op jit(solution)/shard_map/reduce_scatter | solution.py:48
  (2 shorter events, 0.0 us)
Async XLA Ops:
  6.5 88.2 %all-gather.4.cloned.1.call-start = ((), (), s32[]{:S(2)}) async-start(), calls=%async_computation.2 | async-start | bytes 6217728 | tf_op jit(solution)/shard_map/all_gather | solution.py:40
  7.3 176.0 %reduce-scatter.5.cloned.1.call-start = ((), (), s32[]{:S(2)}) async-start(), calls=%async_computation.3 | async-start | bytes 7372800 | tf_op jit(solution)/shard_map/reduce_scatter | solution.py:47
  119.2 101.0 %reduce-scatter.7.cloned.1.call-start = ((), (), s32[]{:S(2)}) async-start(), calls=%async_computation.4 | async-start | bytes 1695744 | tf_op jit(solution)/shard_map/reduce_scatter | solution.py:48
Sparse Core Ops, SparseCore 0:
  10.2 70.8 all-gather.3
  119.3 63.9 reduce-scatter.4
  186.0 34.1 reduce-scatter.6
where the time goes:
time: 227 us
  waiting for transfers between devices  99.1 us (44%)
  blocking collectives  82 us (36%)
  matrix products  24.4 us (11%)
  between operations  14.4 us (6%)
  other arithmetic  3.78 us (2%)
  local copies, waits for them, and re-layouts  2.97 us (1%)
    reduce_scatter x1, waiting for transfers between devices, on_device(): share = lax.psum_scatter(share, 'attn', scatter_dimension=0, tiled=True)  64.1 us
    all_gather x1, blocking collectives, on_device(): all_ids = lax.all_gather(expert_ids, both, axis=0, tiled=True)  44.1 us
    all_gather x1, blocking collectives, on_device(): all_probs = lax.all_gather(gate_probs, both, axis=0, tiled=True)  37.9 us
    reduce_scatter x1, waiting for transfers between devices, on_device(): return lax.psum_scatter(share, 'expert', scatter_dimension=0, tiled=True)  34.3 us
    dot_general x1, matrix products, on_device(): jnp.dot(hidden, down_weight[0], preferred_element_type=jnp.float32)  16.3 us
    dot_general x1, matrix products, on_device(): up_part = jnp.dot(rows, up_weight[0], preferred_element_type=jnp.float32)  8.09 us
  transfers between devices with their start and end apart: 3, of which 2 were waited for; matrix products, arithmetic and copies ran while one was open for 2% of the time, Pallas kernels for 0%

commit v1 on v0

--- a/solution.py
+++ b/solution.py
@@ -36,8 +36,11 @@
     block_size = capacity // 8
     both = ("attn", "expert")
     all_ids = lax.all_gather(expert_ids, both, axis=0, tiled=True)
-    all_probs = lax.all_gather(gate_probs, both, axis=0, tiled=True)
-    rows = lax.all_gather(tokens, both, axis=0, tiled=True)
+    all_probs, rows = jnp.split(
+        lax.all_gather(jnp.concatenate([gate_probs, tokens], axis=1), both, axis=0, tiled=True),
+        [gate_probs.shape[1]],
+        axis=1,
+    )
     weight = row_weights(all_ids, all_probs, shed_blocks, partner, capacity, block_size)
     gate_part = jnp.dot(rows, gate_weight[0], preferred_element_type=jnp.float32)
     up_part = jnp.dot(rows, up_weight[0], preferred_element_type=jnp.float32)

time: 227 us -> 244 us (1.075)
  waiting for transfers between devices: 99.1 us -> 147 us
  blocking collectives: 82 us -> 44.5 us
  matrix products: 24.4 us -> 27.3 us
    all_gather x1, waiting for transfers between devices: 0.01 us -> 47.1 us  [on_device(): lax.all_gather(jnp.concatenate([gate_probs, tokens], axis=1), both, axis=...]
    all_gather x1 -> x0, blocking collectives: 37.9 us -> none  [on_device(): all_probs = lax.all_gather(gate_probs, both, axis=0, tiled=True)]
    dot_general x0 -> x1, matrix products: none -> 11.2 us  [on_device(): jnp.dot(rows, gate_weight[0], preferred_element_type=jnp.float32)]
    dot_general x1, matrix products: 16.3 us -> 6.89 us  [on_device(): jnp.dot(hidden, down_weight[0], preferred_element_type=jnp.float32)]
  transfers between devices with their start and end apart: 3 -> 3, of which waited for: 2 -> 3; matrix products, arithmetic and copies ran while one was open for 2% -> 2% of each run, Pallas kernels for 0% -> 0%
where the time goes in v1:
time: 244 us
  waiting for transfers between devices  147 us (60%)
  blocking collectives  44.5 us (18%)
  matrix products  27.3 us (11%)
  between operations  14.4 us (6%)
  other arithmetic  5.57 us (2%)
  local copies, waits for them, and re-layouts  5.05 us (2%)
    reduce_scatter x1, waiting for transfers between devices, on_device(): share = lax.psum_scatter(share, 'attn', scatter_dimension=0, tiled=True)  65.5 us
    all_gather x1, waiting for transfers between devices, on_device(): lax.all_gather(jnp.concatenate([gate_probs, tokens], axis=1), both, axis=...  47.1 us
    all_gather x1, blocking collectives, on_device(): all_ids = lax.all_gather(expert_ids, both, axis=0, tiled=True)  44.5 us
    reduce_scatter x1, waiting for transfers between devices, on_device(): return lax.psum_scatter(share, 'expert', scatter_dimension=0, tiled=True)  34.3 us
    dot_general x1, matrix products, on_device(): jnp.dot(rows, gate_weight[0], preferred_element_type=jnp.float32)  11.2 us
    dot_general x1, matrix products, on_device(): up_part = jnp.dot(rows, up_weight[0], preferred_element_type=jnp.float32)  9.24 us
    dot_general x1, matrix products, on_device(): jnp.dot(hidden, down_weight[0], preferred_element_type=jnp.float32)  6.89 us
  transfers between devices with their start and end apart: 3, of which 3 were waited for; matrix products, arithmetic and copies ran while one was open for 2% of the time, Pallas kernels for 0%

profile of v1, /device:TPU:0, one launch (start us, length us, event | category | flops | bytes accessed | tf_op | source)
XLA Modules:
  0.0 243.8 jit_solution(16755906126565816000)
XLA Ops:
  6.5 0.0 all-gather.3.cloned.1.call-start
  6.5 0.8 copy.14
  7.3 0.9 convert_element_type.22
  8.3 0.9 pad_maximum_fusion
  9.1 0.0 all-gather.3.cloned.1.call-update
  9.2 0.0 reduce-scatter.5.cloned.1.call-start
  9.2 44.5 %all-gather = s32[32,32,4]{1,2,0:T(4,128)S(1)} all-gather(s32[1,32,4]{1,2,0:T(4,128)} %bitcast.22), channel_id=1, replica_groups=mesh['attn'=4,'expert'=8] {'attn','expert'}, dimensions={0}, use_global_device_ids=true | all-gather | bytes 16896 | tf_op jit(solution)/shard_map/all_gather | solution.py:38
  53.7 0.1 fusion.16
  53.8 0.1 reshape.58
  53.9 0.1 reshape.64
  54.0 1.3 fusion.13
  55.3 1.9 fusion.14
  58.4 0.3 reduce-window.9
  58.7 0.1 slice.7
  58.8 0.1 reshape.62
  58.9 0.1 slice_reduce_fusion
  59.0 47.1 %all-gather.3.cloned.1.call-done = f32[1024,2884]{1,0:T(8,128)} async-done(((f32[32,2884]{1,0:T(8,128)}), f32[1024,2884]{1,0:T(8,128)}) %all-gather.3.cloned.1.call-update) | async-done | bytes 11812880 | tf_op jit(solution)/shard_map/all_gather | solution.py:40
  106.1 1.1 split.9
  107.2 0.2 copy.20
  107.4 0.1 fusion.12
  107.5 0.0 slice-start
  107.5 9.2 %fusion = f32[1024,720]{0,1:T(8,128)S(1)} fusion(f32[1024,2884]{1,0:T(8,128)} %all-gather.3.cloned.1.call-done, bf16[1,2880,720]{1,2,0:T(8,128)(2,1)} %param.14), kind=kOutput, calls=%fused_computation | convolution fusion | flops 4246732800 | bytes 13217792 | tf_op jit(solution)/shard_map/dot_general | solution.py:46
  116.8 0.0 slice-start.1
  116.8 11.2 %multiply_convert_fusion = bf16[1024,720]{0,1:T(8,128)(2,1)S(1)} fusion(f32[1024,720]{0,1:T(8,128)S(1)} %fusion, bf16[1,2880,720]{1,2,0:T(8,128)(2,1)} %param.13, f32[1024,2884]{1,0:T(8,128)} %all-gather.3.cloned.1.call-done, f32[1024]{0:T(1024)S(1)} %fusion.12), kind=kOutput, calls=%fused_computation.8 | convolution fusion | flops 4253368320 | bytes 14696448 | tf_op jit(solution)/shard_map/dot_general | solution.py:45
  128.0 0.0 slice-done
  128.0 0.0 slice-done.1
  128.0 6.9 %convolution_convert_fusion = bf16[1024,2880]{0,1:T(8,128)(2,1)} fusion(bf16[1024,720]{0,1:T(8,128)(2,1)S(1)} %multiply_convert_fusion, bf16[1,720,2880]{2,1,0:T(8,128)(2,1)S(1)} %bitcast.24), kind=kOutput, calls=%fused_computation.4 | convolution fusion | flops 4249681920 | bytes 11520000 | tf_op jit(solution)/shard_map/dot_general | solution.py:49
  134.9 0.0 reduce-scatter.5.cloned.1.call-update
  134.9 0.0 reduce-scatter.7.cloned.1.call-start
  135.0 65.5 %reduce-scatter.5.cloned.1.call-done = bf16[256,2880]{0,1:T(8,128)(2,1)} async-done(((bf16[1024,2880]{0,1:T(8,128)(2,1)}), bf16[256,2880]{0,1:T(8,128)(2,1)}) %reduce-scatter.5.cloned.1.call-update) | async-done | bytes 1474576 | tf_op jit(solution)/shard_map/reduce_scatter | solution.py:50
  200.4 2.6 %copy.18 = bf16[256,2880]{1,0:T(8,128)(2,1)} copy(bf16[256,2880]{0,1:T(8,128)(2,1)} %reduce-scatter.5.cloned.1.call-done) | data formatting | bytes 2949120
  203.0 0.0 reduce-scatter.7.cloned.1.call-update
  203.0 34.3 %reduce-scatter.7.cloned.1.call-done = bf16[32,2880]{1,0:T(8,128)(2,1)} async-done(((bf16[256,2880]{1,0:T(8,128)(2,1)}), bf16[32,2880]{1,0:T(8,128)(2,1)}) %reduce-scatter.7.cloned.1.call-update) | async-done | bytes 184336 | tf_op jit(solution)/shard_map/reduce_scatter | solution.py:51
  (5 shorter events, 0.1 us)
Async XLA Ops:
  6.5 99.6 %all-gather.3.cloned.1.call-start = ((), (), s32[]{:S(2)}) async-start(), calls=%async_computation.2 | async-start | bytes 12435456 | tf_op jit(solution)/shard_map/all_gather | solution.py:40
  9.2 191.2 %reduce-scatter.5.cloned.1.call-start = ((), (), s32[]{:S(2)}) async-start(), calls=%async_computation.3 | async-start | bytes 7372800 | tf_op jit(solution)/shard_map/reduce_scatter | solution.py:50
  107.5 20.5 %slice-start = ((s8[4239360]{0:T(1024)(128)(4,1)}), s8[4194304]{0:T(1024)(128)(4,1)S(1)}, s32[]{:S(2)}) async-start(s8[4239360]{0:T(1024)(128)(4,1)} %bitcast.23), calls=%async_computation.5 | async-start | bytes 8388608
  116.8 11.2 %slice-start.1 = ((s8[4239360]{0:T(1024)(128)(4,1)}), s8[45056]{0:T(1024)(128)(4,1)S(1)}, s32[]{:S(2)}) async-start(s8[4239360]{0:T(1024)(128)(4,1)} %bitcast.23), calls=%async_computation.6 | async-start | bytes 90112
  134.9 102.4 %reduce-scatter.7.cloned.1.call-start = ((), (), s32[]{:S(2)}) async-start(), calls=%async_computation.4 | async-start | bytes 1695744 | tf_op jit(solution)/shard_map/reduce_scatter | solution.py:51
Sparse Core Ops, SparseCore 0:
  10.2 95.9 all-gather.2
  135.0 65.3 reduce-scatter.4
  203.1 34.1 reduce-scatter.6
